TPU v7x, 512 devices: a whole 4x4x16 slice. The times are simulated.
512 devices in a mesh: cuts: 32 (over x, y, core), tr: 16 (over z).
Axes of the slice: x: 4, y: 4, z: 16, core: 2. Of those that a mesh axis runs over, the one named last changes fastest.
Arguments:
- cells: int32 [2, 32, 2, 1024], P(None, 'cuts'), may hold values from 1 to 509
- offsets: float32 [2, 32, 2, 1024], P(None, 'cuts'), may hold values from 0 to 1
- charges: float32 [2, 32, 1024], P(None, 'cuts'), may hold values from 0.5 to 2
- momenta: float32 [2, 32, 2, 1024], P(None, 'cuts', None, 'tr'), may hold values from -6 to 6
- green: float32 [1024, 1024], replicated, may hold values from -0.1875 to 0.1875
Outputs:
- momenta_out: float32 [2, 32, 2, 1024], P(None, 'cuts', None, 'tr')
Inputs may be any that keep to these rules, and one draw needn't show every extreme that they name: `cells`: every cell index lies in 1 .. 509.
All inputs are finite; a program needn't handle non-finite values.
Results may differ from a plain program's by a relative error of at most 0.017.
Values may be sent and summed in bfloat16 or wider, within the bound.
A program may use at most 64 MiB of HBM per device.

v0:
```python
import math
import jax
import jax.numpy as jnp
from jax import lax
from jax.sharding import PartitionSpec as P

SECTIONS = 4
drift_step = 0.5


def padded(cells, sides, width):
    for axis, dim in sides:
        count = lax.axis_size(axis)
        ends = count - 1
        head = lax.slice_in_dim(cells, 0, width, axis=dim)
        tail = lax.slice_in_dim(cells, cells.shape[dim] - width, cells.shape[dim], axis=dim)
        cells = jnp.concatenate(
            [
                lax.ppermute(tail, axis, [(i, (i + 1) % count) for i in range(ends)]),
                cells,
                lax.ppermute(head, axis, [((i + 1) % count, i) for i in range(ends)]),
            ],
            axis=dim,
        )
    return cells


def shifted(value, axis, steps):
    count = lax.axis_size(axis)
    pairs = [(source, (source + steps) % count) for source in range(count)]
    return lax.ppermute(value, axis, pairs)


def split_up(x, dim, count):
    shape = x.shape
    tiles = x.reshape(*shape[:dim], count, shape[dim] // count, *shape[dim + 1 :])
    return jnp.moveaxis(tiles, dim, 0)


def sent_and_summed(x, axis, dim):
    count = lax.axis_size(axis)
    tiles = lax.all_to_all(split_up(x, dim, count), axis, 0, 0, tiled=True)
    return jnp.sum(tiles, axis=0)


def in_order(tiles, dim):
    shape = list(tiles.shape[1:])
    shape[dim] *= tiles.shape[0]
    return jnp.moveaxis(tiles, 0, dim).reshape(shape)


def copy_for_each(x, axis):
    count = lax.axis_size(axis)
    return lax.all_to_all(jnp.broadcast_to(x[None], (count, *x.shape)), axis, 0, 0, tiled=True)


def gather_directly(x, axis, dim):
    return in_order(copy_for_each(x, axis), dim)


def phase_angles(frequency, position, period):
    return 2.0 * math.pi / period * (frequency * position % period).astype(jnp.float32)


def column_table(inputs, with_imag, begin_col, col_count, piece_width, period):
    columns = begin_col + lax.iota(jnp.int32, col_count)
    halves = columns // piece_width % 2
    frequency = columns // (2 * piece_width) * piece_width + columns % piece_width
    position = lax.iota(jnp.int32, inputs)[:, None]
    theta = phase_angles(frequency[None, :], position, period)
    cosine = jnp.cos(theta)
    sine = jnp.sin(theta)
    table = jnp.where(halves[None, :] == 0, cosine, -sine)
    if with_imag:
        lower = jnp.where(halves[None, :] == 0, sine, cosine)
        table = jnp.concatenate([table, lower], axis=0)
    return table.astype(jnp.bfloat16)


def row_table(inputs, period):
    theta = phase_angles(
        lax.iota(jnp.int32, period)[:, None], lax.iota(jnp.int32, inputs)[None, :], period
    )
    return jnp.concatenate([jnp.cos(theta), jnp.sin(theta)], axis=0).astype(jnp.bfloat16)


def forward_rows(table, spectrum, piece_width):
    both_parts = jnp.dot(table, spectrum, preferred_element_type=jnp.float32)
    period = table.shape[0] // 2
    cosine_part = both_parts[:period]
    sine_part = both_parts[period:]
    real_part = cosine_part[:, :piece_width] + sine_part[:, piece_width:]
    imag_part = cosine_part[:, piece_width:] - sine_part[:, :piece_width]
    return (real_part, imag_part)


def hat_weights(cells_along, fraction, first_node, node_count):
    nodes = first_node + lax.iota(jnp.int32, node_count)[None, :]
    lower = jnp.where(cells_along[:, None] == nodes, 1.0 - fraction[:, None], 0.0)
    upper = jnp.where(cells_along[:, None] + 1 == nodes, fraction[:, None], 0.0)
    return lower + upper


def deposit(cells, offsets, charges, first_node, node_rows, node_cols):
    particles = cells.shape[1]
    block_size = math.gcd(particles, 512)
    grid_sum = jnp.zeros((node_rows, node_cols), jnp.float32)
    for number in range(particles // block_size):
        begin_at = number * block_size
        finish_at = begin_at + block_size
        weight_rows = hat_weights(
            cells[0, begin_at:finish_at], offsets[0, begin_at:finish_at], first_node, node_rows
        )
        weight_cols = hat_weights(
            cells[1, begin_at:finish_at], offsets[1, begin_at:finish_at], 0, node_cols
        )
        weight_cols = charges[begin_at:finish_at][:, None] * weight_cols
        grid_sum = grid_sum + lax.dot_general(
            weight_rows.astype(jnp.bfloat16),
            weight_cols.astype(jnp.bfloat16),
            (((0,), (0,)), ((), ())),
            preferred_element_type=jnp.float32,
        )
    return grid_sum.astype(jnp.bfloat16)


def drift(cells, offsets, moment, extent):
    place = cells.astype(jnp.float32) + offsets + drift_step * moment
    place = jnp.clip(place, 1.0, extent - 2.0 - 1.0 / 64.0)
    whole = jnp.floor(place)
    return (whole.astype(jnp.int32), place - whole)


def potentials(pair_grid, pair_columns, own_columns, pair_rows, kernel_re, kernel_im, piece_width):
    spectrum = jnp.dot(pair_grid, own_columns, preferred_element_type=jnp.float32).astype(
        jnp.bfloat16
    )
    forward_re, forward_im = forward_rows(pair_rows, spectrum, piece_width)
    scaled = jnp.concatenate(
        [
            forward_re * kernel_re - forward_im * kernel_im,
            forward_re * kernel_im + forward_im * kernel_re,
        ],
        axis=1,
    ).astype(jnp.bfloat16)
    period = pair_rows.shape[0] // 2
    extent = pair_rows.shape[1]
    halves = lax.dot_general(
        pair_rows.reshape(2, period, extent),
        scaled,
        (((1,), (0,)), ((), ())),
        preferred_element_type=jnp.float32,
    )
    cosine_part = halves[0]
    sine_part = halves[1]
    inverse = jnp.concatenate(
        [
            cosine_part[:, :piece_width] - sine_part[:, piece_width:],
            cosine_part[:, piece_width:] + sine_part[:, :piece_width],
        ],
        axis=1,
    ).astype(jnp.bfloat16)
    inverse = lax.all_to_all(inverse, "tr", split_axis=0, concat_axis=1, tiled=True)
    potential = lax.dot_general(
        inverse, pair_columns, (((1,), (1,)), ((), ())), preferred_element_type=jnp.float32
    ) * (1.0 / (period * period))
    return potential.reshape(potential.shape[0], 2, extent)


def field_grids(potential):
    widened = padded(potential.astype(jnp.bfloat16), (("tr", 0),), 1).astype(potential.dtype)
    along_rows = (widened[:-2] - widened[2:]) * 0.5
    sideways = jnp.pad(potential, ((0, 0), (0, 0), (1, 1)))
    along_cols = (sideways[:, :, :-2] - sideways[:, :, 2:]) * 0.5
    stacked = jnp.stack([along_rows, along_cols], axis=0)
    node_rows = potential.shape[0]
    return (
        jnp.transpose(stacked, (2, 0, 1, 3))
        .reshape(2, 2 * node_rows, potential.shape[2])
        .astype(jnp.bfloat16)
    )


def kick_terms(cells, offsets, fields, first_node, node_rows, row_count):
    node_cols = fields.shape[2]
    block_size = math.gcd(row_count, 256)

    def one_block(number):
        begin_at = number * block_size
        columns = []
        for beam_index in range(2):
            row_cells = lax.dynamic_slice_in_dim(cells[beam_index, 0], begin_at, block_size)
            col_cells = lax.dynamic_slice_in_dim(cells[beam_index, 1], begin_at, block_size)
            row_frac = lax.dynamic_slice_in_dim(offsets[beam_index, 0], begin_at, block_size)
            col_frac = lax.dynamic_slice_in_dim(offsets[beam_index, 1], begin_at, block_size)
            weight_rows = hat_weights(row_cells, row_frac, first_node, node_rows).astype(
                jnp.bfloat16
            )
            weight_cols = hat_weights(col_cells, col_frac, 0, node_cols).astype(jnp.bfloat16)
            projected = lax.dot_general(
                weight_cols,
                fields[1 - beam_index],
                (((1,), (1,)), ((), ())),
                preferred_element_type=jnp.float32,
            )
            projected = projected.reshape(block_size, 2, node_rows)
            columns.append(jnp.sum(projected * weight_rows.astype(jnp.float32)[:, None, :], axis=2))
        return jnp.concatenate(columns, axis=1)

    blocks = lax.map(one_block, jnp.arange(row_count // block_size, dtype=jnp.int32))
    return blocks.reshape(row_count, 4)


def per_device(cells, offsets, charges, momenta, green):
    shards = lax.axis_size("tr")
    shard_index = lax.axis_index("tr")
    period = green.shape[0]
    extent = period // 2
    node_rows = extent // shards
    piece_width = period // shards
    first_node = shard_index * node_rows
    kernel_columns = column_table(
        period, False, shard_index * 2 * piece_width, 2 * piece_width, piece_width, period
    )
    kernel_cols = jnp.dot(
        green.astype(jnp.bfloat16), kernel_columns, preferred_element_type=jnp.float32
    ).astype(jnp.bfloat16)
    kernel_re, kernel_im = forward_rows(row_table(period, period), kernel_cols, piece_width)
    pair_columns = column_table(extent, True, 0, 2 * period, piece_width, period)
    pair_rows = row_table(extent, period)
    own_columns = column_table(
        extent, True, shard_index * 2 * piece_width, 2 * piece_width, piece_width, period
    )
    deposit_first = 0
    local_cells = cells[:, 0]
    local_offsets = offsets[:, 0]
    local_charges = charges[:, 0]
    moment = momenta
    particle_rows = momenta.shape[-1]
    for section_index in range(SECTIONS):
        charge_grids = [
            deposit(
                local_cells[beam_index],
                local_offsets[beam_index],
                local_charges[beam_index],
                deposit_first,
                extent,
                extent,
            )
            for beam_index in range(2)
        ]
        if section_index > 0:
            charge_grids = [
                shifted(charge_grids[0], "cuts", 2 * section_index),
                shifted(charge_grids[1], "cuts", -2 * section_index),
            ]
        pair_grid = jnp.concatenate(charge_grids, axis=1)
        potential = potentials(
            pair_grid, pair_columns, own_columns, pair_rows, kernel_re, kernel_im, piece_width
        )
        fields = field_grids(potential)
        kick_sums = sent_and_summed(
            kick_terms(
                local_cells,
                local_offsets,
                fields,
                first_node,
                node_rows,
                particle_rows * lax.axis_size("tr"),
            ),
            "tr",
            0,
        )
        moment = moment + jnp.transpose(kick_sums).reshape(moment.shape)
        if section_index + 1 < SECTIONS:
            whole_moment = gather_directly(moment, "tr", 3)
            local_cells, local_offsets = drift(
                local_cells, local_offsets, whole_moment[:, 0], extent
            )
    return moment


def solution(mesh):
    return jax.shard_map(
        per_device,
        mesh=mesh,
        in_specs=(
            P(None, "cuts", None, None),
            P(None, "cuts", None, None),
            P(None, "cuts", None),
            P(None, "cuts", None, "tr"),
            P(),
        ),
        out_specs=P(None, "cuts", None, "tr"),
        check_vma=False,
    )
```

profile of v0, /device:TPU:6, one launch (start us, length us, event | category | flops | bytes accessed | tf_op | source)
XLA Modules:
  0.0 439.0 jit_solution(6951870104126059463)
XLA Ops:
  0.0 8.5 %fusion.147 = (bf16[1024,512]{1,0:T(8,128)(2,1)S(1)}, bf16[1024,512]{1,0:T(8,128)(2,1)S(1)}) fusion(), kind=kLoop, calls=%fused_computation.362 | loop fusion | flops 8388608 | bytes 2097152 | tf_op jit(solution)/shard_map/sin | solution.py:84
  8.6 17.7 %sine_convert_fusion = (bf16[1024,1024]{1,0:T(8,128)(2,1)}, bf16[1024,1024]{1,0:T(8,128)(2,1)}) fusion(), kind=kLoop, calls=%fused_computation.206 | loop fusion | flops 16777216 | bytes 4194304 | tf_op jit(solution)/shard_map/convert.43
  28.2 8.5 %fusion.86 = f32[2048,128]{0,1:T(8,128)} fusion(bf16[1024,1024]{1,0:T(8,128)(2,1)} %get-tuple-element.438, bf16[1024,1024]{1,0:T(8,128)(2,1)} %get-tuple-element.439, f32[1024,1024]{1,0:T(8,128)} %param.17, s32[128]{0:T(128)S(1)} %fusion.412, pred[128]{0:T(512)(128)(4,1)S(1)} %fusion.413), kind=kOutput, calls=%fused_computation.197 | convolution fusion | flops 817102848 | bytes 9437824 | tf_op jit(solution)/shard_map/dot_general | solution.py:88
  49.1 15.7 %all-to-all-start = ((bf16[16,32,128]{2,1,0:T(8,128)(2,1)}), bf16[16,32,128]{2,1,0:T(8,128)(2,1)S(1)}, u32[]{:S(2)}, u32[]{:S(2)}) async-start(bf16[16,32,128]{2,1,0:T(8,128)(2,1)} %pad_maximum_fusion.2), calls=%async_computation | async-start | bytes 262144 | tf_op jit(solution)/shard_map/all_to_all | solution.py:163
  64.9 18.5 %select_convert_fusion.1 = (bf16[512,2048]{1,0:T(8,128)(2,1)}, bf16[512,2048]{1,0:T(8,128)(2,1)}) fusion(s32[2048]{0:T(1024)S(1)} %fusion.409, pred[2048]{0:T(1024)(128)(4,1)S(1)} %fusion.406), kind=kLoop, calls=%fused_computation.203 | loop fusion | flops 19922944 | bytes 4204544 | tf_op jit(solution)/shard_map/convert.34
  87.5 3.9 collective-permute-start
  92.7 4.2 collective-permute-done.1
  97.3 9.5 %while.40 = (s32[]{:T(128)}, f32[4,256,4]{1,0,2:T(4,128)S(1)}, s32[2,2,1024]{2,1,0:T(2,128)S(1)}, s32[4]{0:T(128)S(1)}, f32[2,2,1024]{2,1,0:T(2,128)S(1)}, /*ind...) while((s32[]{:T(128)}, f32[4,256,4]{1,0,2:T(4,128)S(1)}, ...), condition=%wide.region_3.4_spmd, body=%wide.region_0.3_spmd.sunk | while | flops 35309604 | bytes 668095 | solution.py:210
  107.0 24.2 %all_to_all.99 = f32[16,1,256]{2,1,0:T(1,128)S(1)} all-to-all(f32[16,1,256]{2,1,0:T(1,128)S(1)} %reshape.1728), channel_id=1, replica_groups=mesh['cuts'=32,'tr'=16] {'tr'}, dimensions={0} | all-to-all | bytes 32768 | tf_op jit(solution)/shard_map/all_to_all | solution.py:42
  132.7 15.0 %all_to_all.100 = f32[16,1,256]{2,1,0:T(1,128)S(1)} all-to-all(f32[16,1,256]{2,1,0:T(1,128)S(1)} %reshape.1730), channel_id=1, replica_groups=mesh['cuts'=32,'tr'=16] {'tr'}, dimensions={0} | all-to-all | bytes 32768 | tf_op jit(solution)/shard_map/all_to_all | solution.py:54
  157.1 4.6 %collective-permute-start.3 = (bf16[512,512]{1,0:T(8,128)(2,1)S(1)}, bf16[512,512]{1,0:T(8,128)(2,1)}, u32[]{:S(2)}, u32[]{:S(2)}) collective-permute-start(bf16[512,512]{1,0:T(8,128)(2,1)S(1)} %fusion.109), channel_id=1, source_target_pairs={{0,480},{16,496},{32,0},{48,16},{64,32},{80,48},{96,64},{112,80},{... | collective-permute-start | bytes 1572872 | tf_op jit(solution)/shard_map/ppermute | solution.py:31
  164.4 4.0 collective-permute-done.3
  168.4 3.8 fusion.118
  174.5 15.9 %all_to_all.101 = bf16[16,32,128]{2,1,0:T(8,128)(2,1)S(1)} all-to-all(bf16[16,32,128]{2,1,0:T(8,128)(2,1)S(1)} %pad_maximum_fusion.3), channel_id=1, replica_groups=mesh['cuts'=32,'tr'=16] {'tr'}, dimensions={0} | all-to-all | bytes 262144 | tf_op jit(solution)/shard_map/all_to_all | solution.py:163
  198.8 4.2 collective-permute-done.5
  203.4 9.6 %while.41 = (s32[]{:T(128)}, f32[4,256,4]{1,0,2:T(4,128)S(1)}, s32[2,2,1024]{2,1,0:T(2,128)S(1)}, s32[4]{0:T(128)S(1)}, f32[2,2,1024]{2,1,0:T(2,128)S(1)}, /*ind...) while((s32[]{:T(128)}, f32[4,256,4]{1,0,2:T(4,128)S(1)}, ...), condition=%wide.region_8.9_spmd, body=%wide.region_5.8_spmd.sunk | while | flops 35309604 | bytes 668095 | solution.py:210
  213.2 18.6 %all_to_all.102 = f32[16,1,256]{2,1,0:T(1,128)S(1)} all-to-all(f32[16,1,256]{2,1,0:T(1,128)S(1)} %reshape.1732), channel_id=1, replica_groups=mesh['cuts'=32,'tr'=16] {'tr'}, dimensions={0} | all-to-all | bytes 32768 | tf_op jit(solution)/shard_map/all_to_all | solution.py:42
  232.6 15.0 %all_to_all.103 = f32[16,1,256]{2,1,0:T(1,128)S(1)} all-to-all(f32[16,1,256]{2,1,0:T(1,128)S(1)} %reshape.1734), channel_id=1, replica_groups=mesh['cuts'=32,'tr'=16] {'tr'}, dimensions={0} | all-to-all | bytes 32768 | tf_op jit(solution)/shard_map/all_to_all | solution.py:54
  251.0 4.8 %collective-permute-start.6 = (bf16[512,512]{1,0:T(8,128)(2,1)S(1)}, bf16[512,512]{1,0:T(8,128)(2,1)}, u32[]{:S(2)}, u32[]{:S(2)}) collective-permute-start(bf16[512,512]{1,0:T(8,128)(2,1)S(1)} %fusion.110), channel_id=1, source_target_pairs={{0,64},{16,80},{32,96},{48,112},{64,128},{80,144},{96,160},{112,17... | collective-permute-start | bytes 1572872 | tf_op jit(solution)/shard_map/ppermute | solution.py:31
  264.6 6.4 %collective-permute-done.7 = bf16[512,512]{1,0:T(8,128)(2,1)} collective-permute-done((bf16[512,512]{1,0:T(8,128)(2,1)S(1)}, bf16[512,512]{1,0:T(8,128)(2,1)}, u32[]{:S(2)}, u32[]{:S(2)}) %collective-permute-start.7) | collective-permute-done | bytes 524320 | tf_op jit(solution)/shard_map/ppermute | solution.py:31
  270.9 3.8 fusion.119
  277.0 15.7 %all_to_all.104 = bf16[16,32,128]{2,1,0:T(8,128)(2,1)S(1)} all-to-all(bf16[16,32,128]{2,1,0:T(8,128)(2,1)S(1)} %pad_maximum_fusion.4), channel_id=1, replica_groups=mesh['cuts'=32,'tr'=16] {'tr'}, dimensions={0} | all-to-all | bytes 262144 | tf_op jit(solution)/shard_map/all_to_all | solution.py:163
  301.1 4.2 collective-permute-done.9
  305.7 9.8 %while.42 = (s32[]{:T(128)}, f32[4,256,4]{1,0,2:T(4,128)S(1)}, s32[2,2,1024]{2,1,0:T(2,128)S(1)}, s32[4]{0:T(128)S(1)}, f32[2,2,1024]{2,1,0:T(2,128)S(1)}, /*ind...) while((s32[]{:T(128)}, f32[4,256,4]{1,0,2:T(4,128)S(1)}, ...), condition=%wide.region_13.14_spmd, body=%wide.region_10.13_spmd.sunk | while | flops 35309604 | bytes 668095 | solution.py:210
  315.6 18.7 %all_to_all.105 = f32[16,1,256]{2,1,0:T(1,128)S(1)} all-to-all(f32[16,1,256]{2,1,0:T(1,128)S(1)} %reshape.1736), channel_id=1, replica_groups=mesh['cuts'=32,'tr'=16] {'tr'}, dimensions={0} | all-to-all | bytes 32768 | tf_op jit(solution)/shard_map/all_to_all | solution.py:42
  335.2 15.0 %all_to_all.106 = f32[16,1,256]{2,1,0:T(1,128)S(1)} all-to-all(f32[16,1,256]{2,1,0:T(1,128)S(1)} %reshape.1738), channel_id=1, replica_groups=mesh['cuts'=32,'tr'=16] {'tr'}, dimensions={0} | all-to-all | bytes 32768 | tf_op jit(solution)/shard_map/all_to_all | solution.py:54
  353.6 6.0 %collective-permute-start.10 = (bf16[512,512]{1,0:T(8,128)(2,1)S(1)}, bf16[512,512]{1,0:T(8,128)(2,1)S(1)}, u32[]{:S(2)}, u32[]{:S(2)}) collective-permute-start(bf16[512,512]{1,0:T(8,128)(2,1)S(1)} %fusion.112), channel_id=1, source_target_pairs={{0,96},{16,112},{32,128},{48,144},{64,160},{80,176},{96,192},{112,... | collective-permute-start | bytes 1572872 | tf_op jit(solution)/shard_map/ppermute | solution.py:31
  366.3 8.2 %collective-permute-done.11 = bf16[512,512]{1,0:T(8,128)(2,1)} collective-permute-done((bf16[512,512]{1,0:T(8,128)(2,1)S(1)}, bf16[512,512]{1,0:T(8,128)(2,1)}, u32[]{:S(2)}, u32[]{:S(2)}) %collective-permute-start.11) | collective-permute-done | bytes 524320 | tf_op jit(solution)/shard_map/ppermute | solution.py:31
  380.4 15.8 %all_to_all.107 = bf16[16,32,128]{2,1,0:T(8,128)(2,1)S(1)} all-to-all(bf16[16,32,128]{2,1,0:T(8,128)(2,1)S(1)} %pad_maximum_fusion.5), channel_id=1, replica_groups=mesh['cuts'=32,'tr'=16] {'tr'}, dimensions={0} | all-to-all | bytes 262144 | tf_op jit(solution)/shard_map/all_to_all | solution.py:163
  404.0 4.2 collective-permute-done.13
  408.5 10.0 %while.43 = (s32[]{:T(128)}, f32[4,256,4]{1,0,2:T(4,128)S(1)}, s32[2,2,1024]{2,1,0:T(2,128)S(1)}, s32[4]{0:T(128)S(1)}, f32[2,2,1024]{2,1,0:T(2,128)S(1)}, /*ind...) while((s32[]{:T(128)}, f32[4,256,4]{1,0,2:T(4,128)S(1)}, ...), condition=%wide.region_18.19_spmd, body=%wide.region_15.18_spmd.sunk | while | flops 35309604 | bytes 668095 | solution.py:210
  418.8 18.7 %all_to_all.108 = f32[16,1,256]{2,1,0:T(1,128)S(1)} all-to-all(f32[16,1,256]{2,1,0:T(1,128)S(1)} %reshape.1740), channel_id=1, replica_groups=mesh['cuts'=32,'tr'=16] {'tr'}, dimensions={0} | all-to-all | bytes 32768 | tf_op jit(solution)/shard_map/all_to_all | solution.py:42
  (658 shorter events, 119.9 us)
Async XLA Ops:
  8.5 17.8 %copy-start.5 = (s32[2,1,2,1024]{3,2,1,0:T(2,128)S(1)}, s32[2,1,2,1024]{3,2,1,0:T(2,128)}, u32[]{:S(2)}) copy-start(s32[2,1,2,1024]{3,2,1,0:T(2,128)} %param.13) | copy-start | bytes 49156
  8.5 17.8 %copy-start.6 = (f32[2,1,2,1024]{3,2,1,0:T(2,128)S(1)}, f32[2,1,2,1024]{3,2,1,0:T(2,128)}, u32[]{:S(2)}) copy-start(f32[2,1,2,1024]{3,2,1,0:T(2,128)} %param.14) | copy-start | bytes 49156
  8.6 17.9 %copy-start.8 = (f32[2,1,1024]{2,1,0:T(1,128)S(1)}, f32[2,1,1024]{2,1,0:T(1,128)}, u32[]{:S(2)}) copy-start(f32[2,1,1024]{2,1,0:T(1,128)} %param.15) | copy-start | bytes 24580
  26.4 10.3 %copy-start.16 = (f32[1,1,512]{2,1,0:T(1,128)}, f32[1,1,512]{2,1,0:T(1,128)S(1)}, u32[]{:S(2)}) copy-start(f32[1,1,512]{2,1,0:T(1,128)S(1)} %get-tuple-element.415) | copy-start | bytes 6148
  26.4 11.5 %copy-start.12 = (f32[1,1,512]{2,1,0:T(1,128)}, f32[1,1,512]{2,1,0:T(1,128)S(1)}, u32[]{:S(2)}) copy-start(f32[1,1,512]{2,1,0:T(1,128)S(1)} %get-tuple-element.417) | copy-start | bytes 6148
  26.5 12.7 %copy-start.14 = (f32[1,1,512]{2,1,0:T(1,128)}, f32[1,1,512]{2,1,0:T(1,128)S(1)}, u32[]{:S(2)}) copy-start(f32[1,1,512]{2,1,0:T(1,128)S(1)} %get-tuple-element.414) | copy-start | bytes 6148
  26.5 14.7 %copy-start.10 = (f32[1,1,512]{2,1,0:T(1,128)}, f32[1,1,512]{2,1,0:T(1,128)S(1)}, u32[]{:S(2)}) copy-start(f32[1,1,512]{2,1,0:T(1,128)S(1)} %get-tuple-element.416) | copy-start | bytes 6148
  28.1 15.1 %copy-start.2 = (bf16[512,128]{1,0:T(8,128)(2,1)}, bf16[512,128]{1,0:T(8,128)(2,1)S(1)}, u32[]{:S(2)}) copy-start(bf16[512,128]{1,0:T(8,128)(2,1)S(1)} %get-tuple-element.427) | copy-start | bytes 393220
  49.1 34.2 %all-to-all-start = ((bf16[16,32,128]{2,1,0:T(8,128)(2,1)}), bf16[16,32,128]{2,1,0:T(8,128)(2,1)S(1)}, u32[]{:S(2)}, u32[]{:S(2)}) async-start(bf16[16,32,128]{2,1,0:T(8,128)(2,1)} %pad_maximum_fusion.2), calls=%async_computation | async-start | bytes 262144 | tf_op jit(solution)/shard_map/all_to_all | solution.py:163
  83.4 13.9 %copy-start.7 = (f32[2,1,2,1024]{3,2,1,0:T(2,128)S(1)}, f32[2,1,2,1024]{3,2,1,0:T(2,128)}, u32[]{:S(2)}) copy-start(f32[2,1,2,1024]{3,2,1,0:T(2,128)} %param.14) | copy-start | bytes 49156
  87.5 5.2 %collective-permute-start = (bf16[1,2,512]{2,1,0:T(2,128)(2,1)S(1)}, bf16[1,2,512]{2,1,0:T(2,128)(2,1)S(1)}, u32[]{:S(2)}, u32[]{:S(2)}) collective-permute-start(bf16[1,2,512]{2,1,0:T(2,128)(2,1)S(1)} %get-tuple-element.338), channel_id=1, source_target_pairs={{0,1},{1,2},{2,3},{3,4},{4,5},{5,6},{6,7},{7,8},{8,9},{9,10},{10,1... | collective-permute-start | bytes 6152 | tf_op jit(solution)/shard_map/ppermute | solution.py:19
  91.4 5.5 %collective-permute-start.1 = (bf16[1,2,512]{2,1,0:T(2,128)(2,1)S(1)}, bf16[1,2,512]{2,1,0:T(2,128)(2,1)S(1)}, u32[]{:S(2)}, u32[]{:S(2)}) collective-permute-start(bf16[1,2,512]{2,1,0:T(2,128)(2,1)S(1)} %get-tuple-element.339), channel_id=1, source_target_pairs={{1,0},{2,1},{3,2},{4,3},{5,4},{6,5},{7,6},{8,7},{9,8},{10,9},{11,1... | collective-permute-start | bytes 6152 | tf_op jit(solution)/shard_map/ppermute | solution.py:21
  97.3 35.3 %copy-start.9 = (f32[2,1,2,64]{3,2,1,0:T(2,128)S(1)}, f32[2,1,2,64]{3,2,1,0:T(2,128)}, u32[]{:S(2)}) copy-start(f32[2,1,2,64]{3,2,1,0:T(2,128)} %param.16) | copy-start | bytes 3076
  97.3 51.4 %copy-start.17 = (f32[1,1,512]{2,1,0:T(1,128)S(1)}, f32[1,1,512]{2,1,0:T(1,128)}, u32[]{:S(2)}) copy-start(f32[1,1,512]{2,1,0:T(1,128)} %copy-done.16) | copy-start | bytes 6148
  148.7 1.2 copy-start.15
  149.9 4.8 %copy-start.13 = (f32[1,1,512]{2,1,0:T(1,128)S(1)}, f32[1,1,512]{2,1,0:T(1,128)}, u32[]{:S(2)}) copy-start(f32[1,1,512]{2,1,0:T(1,128)} %copy-done.12) | copy-start | bytes 6148
  151.1 13.3 %collective-permute-start.2 = (bf16[512,512]{1,0:T(8,128)(2,1)S(1)}, bf16[512,512]{1,0:T(8,128)(2,1)}, u32[]{:S(2)}, u32[]{:S(2)}) collective-permute-start(bf16[512,512]{1,0:T(8,128)(2,1)S(1)} %fusion.108), channel_id=1, source_target_pairs={{0,32},{16,48},{32,64},{48,80},{64,96},{80,112},{96,128},{112,144}... | collective-permute-start | bytes 1572872 | tf_op jit(solution)/shard_map/ppermute | solution.py:31
  154.7 1.2 copy-start.11
  155.9 12.5 %copy-start.3 = (bf16[512,128]{1,0:T(8,128)(2,1)S(1)}, bf16[512,128]{1,0:T(8,128)(2,1)}, u32[]{:S(2)}) copy-start(bf16[512,128]{1,0:T(8,128)(2,1)} %copy-done.2) | copy-start | bytes 393220
  157.1 15.2 %copy-start.1 = (f32[1024,64]{0,1:T(8,128)S(1)}, f32[1024,64]{0,1:T(8,128)}, u32[]{:S(2)}) copy-start(f32[1024,64]{0,1:T(8,128)} %copy-done) | copy-start | bytes 786436
  157.1 11.3 %collective-permute-start.3 = (bf16[512,512]{1,0:T(8,128)(2,1)S(1)}, bf16[512,512]{1,0:T(8,128)(2,1)}, u32[]{:S(2)}, u32[]{:S(2)}) collective-permute-start(bf16[512,512]{1,0:T(8,128)(2,1)S(1)} %fusion.109), channel_id=1, source_target_pairs={{0,480},{16,496},{32,0},{48,16},{64,32},{80,48},{96,64},{112,80},{... | collective-permute-start | bytes 1572872 | tf_op jit(solution)/shard_map/ppermute | solution.py:31
  194.5 4.3 collective-permute-start.4
  197.5 5.5 %collective-permute-start.5 = (bf16[1,2,512]{2,1,0:T(2,128)(2,1)S(1)}, bf16[1,2,512]{2,1,0:T(2,128)(2,1)S(1)}, u32[]{:S(2)}, u32[]{:S(2)}) collective-permute-start(bf16[1,2,512]{2,1,0:T(2,128)(2,1)S(1)} %get-tuple-element.337), channel_id=1, source_target_pairs={{1,0},{2,1},{3,2},{4,3},{5,4},{6,5},{7,6},{8,7},{9,8},{10,9},{11,1... | collective-permute-start | bytes 6152 | tf_op jit(solution)/shard_map/ppermute | solution.py:21
  251.0 13.6 %collective-permute-start.6 = (bf16[512,512]{1,0:T(8,128)(2,1)S(1)}, bf16[512,512]{1,0:T(8,128)(2,1)}, u32[]{:S(2)}, u32[]{:S(2)}) collective-permute-start(bf16[512,512]{1,0:T(8,128)(2,1)S(1)} %fusion.110), channel_id=1, source_target_pairs={{0,64},{16,80},{32,96},{48,112},{64,128},{80,144},{96,160},{112,17... | collective-permute-start | bytes 1572872 | tf_op jit(solution)/shard_map/ppermute | solution.py:31
  258.3 12.7 %collective-permute-start.7 = (bf16[512,512]{1,0:T(8,128)(2,1)S(1)}, bf16[512,512]{1,0:T(8,128)(2,1)}, u32[]{:S(2)}, u32[]{:S(2)}) collective-permute-start(bf16[512,512]{1,0:T(8,128)(2,1)S(1)} %fusion.111), channel_id=1, source_target_pairs={{0,448},{16,464},{32,480},{48,496},{64,0},{80,16},{96,32},{112,48}... | collective-permute-start | bytes 1572872 | tf_op jit(solution)/shard_map/ppermute | solution.py:31
  296.8 4.3 collective-permute-start.8
  299.8 5.5 %collective-permute-start.9 = (bf16[1,2,512]{2,1,0:T(2,128)(2,1)S(1)}, bf16[1,2,512]{2,1,0:T(2,128)(2,1)S(1)}, u32[]{:S(2)}, u32[]{:S(2)}) collective-permute-start(bf16[1,2,512]{2,1,0:T(2,128)(2,1)S(1)} %get-tuple-element.335), channel_id=1, source_target_pairs={{1,0},{2,1},{3,2},{4,3},{5,4},{6,5},{7,6},{8,7},{9,8},{10,9},{11,1... | collective-permute-start | bytes 6152 | tf_op jit(solution)/shard_map/ppermute | solution.py:21
  353.6 12.7 %collective-permute-start.10 = (bf16[512,512]{1,0:T(8,128)(2,1)S(1)}, bf16[512,512]{1,0:T(8,128)(2,1)S(1)}, u32[]{:S(2)}, u32[]{:S(2)}) collective-permute-start(bf16[512,512]{1,0:T(8,128)(2,1)S(1)} %fusion.112), channel_id=1, source_target_pairs={{0,96},{16,112},{32,128},{48,144},{64,160},{80,176},{96,192},{112,... | collective-permute-start | bytes 1572872 | tf_op jit(solution)/shard_map/ppermute | solution.py:31
  362.1 12.4 %collective-permute-start.11 = (bf16[512,512]{1,0:T(8,128)(2,1)S(1)}, bf16[512,512]{1,0:T(8,128)(2,1)}, u32[]{:S(2)}, u32[]{:S(2)}) collective-permute-start(bf16[512,512]{1,0:T(8,128)(2,1)S(1)} %fusion.113), channel_id=1, source_target_pairs={{0,416},{16,432},{32,448},{48,464},{64,480},{80,496},{96,0},{112,1... | collective-permute-start | bytes 1572872 | tf_op jit(solution)/shard_map/ppermute | solution.py:31
  379.9 16.3 %copy-start.4 = (bf16[512,2048]{1,0:T(8,128)(2,1)S(1)}, bf16[512,2048]{1,0:T(8,128)(2,1)}, u32[]{:S(2)}) copy-start(bf16[512,2048]{1,0:T(8,128)(2,1)} %get-tuple-element.356) | copy-start | bytes 6291460
  399.6 4.3 collective-permute-start.12
  402.7 5.5 %collective-permute-start.13 = (bf16[1,2,512]{2,1,0:T(2,128)(2,1)S(1)}, bf16[1,2,512]{2,1,0:T(2,128)(2,1)S(1)}, u32[]{:S(2)}, u32[]{:S(2)}) collective-permute-start(bf16[1,2,512]{2,1,0:T(2,128)(2,1)S(1)} %get-tuple-element.333), channel_id=1, source_target_pairs={{1,0},{2,1},{3,2},{4,3},{5,4},{6,5},{7,6},{8,7},{9,8},{10,9},{11,1... | collective-permute-start | bytes 6152 | tf_op jit(solution)/shard_map/ppermute | solution.py:21
  (1 other events, 0.7 us)
where the time goes:
time: 443 us; the launch traced here: 439 us
  blocking collectives  172 us (39%)
  matrix products  69.9 us (16%)
  other arithmetic  63.3 us (14%)
  starting transfers between devices  58.1 us (13%)
  waiting for transfers between devices  43.1 us (10%)
  local copies, waits for them, and re-layouts  16.7 us (4%)
  loops' own time  13.3 us (3%)
    all_to_all x4, blocking collectives, sent_and_summed(): tiles = lax.all_to_all(split_up(x, dim, count), axis, 0, 0, tiled=True)  80.1 us
    all_to_all x3, blocking collectives, potentials(): lax.all_to_all(inverse, 'tr', split_axis=0, concat_axis=1, tiled=True)  47.4 us
    all_to_all x3, blocking collectives, copy_for_each(): lax.all_to_all(jnp.broadcast_to(x[None], (count, *x.shape)), axis, 0, 0,...  44.9 us
    another operation x12, other arithmetic  43.2 us
    ppermute x6, waiting for transfers between devices, shifted(): return lax.ppermute(value, axis, pairs)  26.4 us
    ppermute x6, starting transfers between devices, shifted(): return lax.ppermute(value, axis, pairs)  24.3 us
    dot_general x5, matrix products, forward_rows(): both_parts = jnp.dot(table, spectrum, preferred_element_type=jnp.float32)  22.7 us
    dot_general x16, matrix products, deposit(): lax.dot_general(weight_rows.astype(jnp.bfloat16), weight_cols.astype(jnp....  20.4 us
  transfers between devices with their start and end apart: 15, of which 10 were waited for; matrix products, arithmetic and copies ran while one was open for 6% of the time, Pallas kernels for 0%

commit v1 on v0

--- a/solution.py
+++ b/solution.py
@@ -160,7 +160,10 @@
         ],
         axis=1,
     ).astype(jnp.bfloat16)
-    inverse = lax.all_to_all(inverse, "tr", split_axis=0, concat_axis=1, tiled=True)
+    inverse = jnp.concatenate(
+        lax.all_to_all(jnp.stack(jnp.split(inverse, lax.axis_size("tr"), axis=0)), "tr", 0, 0),
+        axis=1,
+    )
     potential = lax.dot_general(
         inverse, pair_columns, (((1,), (1,)), ((), ())), preferred_element_type=jnp.float32
     ) * (1.0 / (period * period))

time: 443 us -> 463 us (1.045)
  local copies, waits for them, and re-layouts: 16.7 us -> 35.8 us
    unnamed x53 -> x131, local copies, waits for them, and re-layouts: 1.5 us -> 12.2 us
    another operation x12 -> x72, local copies, waits for them, and re-layouts: 0.97 us -> 9.13 us  [the longest x68 9.11 us: potentials(): jnp.stack(jnp.split(inverse, lax.axis_size('tr'), axis=0))]
    another operation x12 -> x20, other arithmetic: 43.2 us -> 45.2 us
where the time goes in v1:
time: 463 us; the launch traced here: 459 us
  blocking collectives  173 us (37%)
  matrix products  69.9 us (15%)
  other arithmetic  64 us (14%)
  starting transfers between devices  58 us (13%)
  waiting for transfers between devices  42.9 us (9%)
  local copies, waits for them, and re-layouts  35.8 us (8%)
  loops' own time  13.4 us (3%)
    all_to_all x4, blocking collectives, sent_and_summed(): tiles = lax.all_to_all(split_up(x, dim, count), axis, 0, 0, tiled=True)  80.1 us
    all_to_all x3, blocking collectives, potentials(): lax.all_to_all(jnp.stack(jnp.split(inverse, lax.axis_size('tr'), axis=0))...  47.5 us
    all_to_all x3, blocking collectives, copy_for_each(): lax.all_to_all(jnp.broadcast_to(x[None], (count, *x.shape)), axis, 0, 0,...  44.9 us
    another operation x12, other arithmetic  43.1 us
    ppermute x6, waiting for transfers between devices, shifted(): return lax.ppermute(value, axis, pairs)  26.4 us
    ppermute x6, starting transfers between devices, shifted(): return lax.ppermute(value, axis, pairs)  24.3 us
    dot_general x5, matrix products, forward_rows(): both_parts = jnp.dot(table, spectrum, preferred_element_type=jnp.float32)  22.7 us
    dot_general x16, matrix products, deposit(): lax.dot_general(weight_rows.astype(jnp.bfloat16), weight_cols.astype(jnp....  20.4 us
  transfers between devices with their start and end apart: 15, of which 10 were waited for; matrix products, arithmetic and copies ran while one was open for 6% of the time, Pallas kernels for 0%

profile of v1, /device:TPU:6, one launch (start us, length us, event | category | flops | bytes accessed | tf_op | source)
XLA Modules:
  0.0 458.9 jit_solution(3666324446381120338)
XLA Ops:
  0.0 8.5 %fusion.147 = (bf16[1024,512]{1,0:T(8,128)(2,1)S(1)}, bf16[1024,512]{1,0:T(8,128)(2,1)S(1)}) fusion(), kind=kLoop, calls=%fused_computation.362 | loop fusion | flops 8388608 | bytes 2097152 | tf_op jit(solution)/shard_map/sin | solution.py:84
  8.6 17.7 %sine_convert_fusion = (bf16[1024,1024]{1,0:T(8,128)(2,1)}, bf16[1024,1024]{1,0:T(8,128)(2,1)}) fusion(), kind=kLoop, calls=%fused_computation.206 | loop fusion | flops 16777216 | bytes 4194304 | tf_op jit(solution)/shard_map/convert.35
  28.1 8.5 %fusion.86 = f32[2048,128]{0,1:T(8,128)} fusion(bf16[1024,1024]{1,0:T(8,128)(2,1)} %get-tuple-element.502, bf16[1024,1024]{1,0:T(8,128)(2,1)} %get-tuple-element.503, f32[1024,1024]{1,0:T(8,128)} %param.17, s32[128]{0:T(128)S(1)} %fusion.536, pred[128]{0:T(512)(128)(4,1)S(1)} %fusion.537), kind=kOutput, calls=%fused_computation.197 | convolution fusion | flops 817102848 | bytes 9437824 | tf_op jit(solution)/shard_map/dot_general | solution.py:88
  59.3 15.4 %all-to-all-start = ((bf16[16,32,128]{2,1,0:T(8,128)(2,1)}), bf16[16,32,128]{2,1,0:T(8,128)(2,1)S(1)}, u32[]{:S(2)}, u32[]{:S(2)}) async-start(bf16[16,32,128]{2,1,0:T(8,128)(2,1)} %constant_dynamic-update-slice_fusion), calls=%async_computation | async-start | bytes 262144 | tf_op jit(solution)/shard_map/all_to_all | solution.py:164
  74.7 18.5 %select_convert_fusion.1 = (bf16[512,2048]{1,0:T(8,128)(2,1)}, bf16[512,2048]{1,0:T(8,128)(2,1)}) fusion(s32[2048]{0:T(1024)S(1)} %fusion.533, pred[2048]{0:T(1024)(128)(4,1)S(1)} %fusion.530), kind=kLoop, calls=%fused_computation.203 | loop fusion | flops 19922944 | bytes 4204544 | tf_op jit(solution)/shard_map/convert.28
  97.3 3.9 collective-permute-start
  102.6 4.2 collective-permute-done.1
  107.2 9.9 %while.40 = (s32[]{:T(128)}, f32[4,256,4]{1,0,2:T(4,128)S(1)}, s32[2,2,1024]{2,1,0:T(2,128)S(1)}, s32[4]{0:T(128)S(1)}, f32[2,2,1024]{2,1,0:T(2,128)S(1)}, /*ind...) while((s32[]{:T(128)}, f32[4,256,4]{1,0,2:T(4,128)S(1)}, ...), condition=%wide.region_3.4_spmd, body=%wide.region_0.3_spmd.sunk | while | flops 35309604 | bytes 668095 | solution.py:213
  117.3 24.2 %all_to_all.55 = f32[16,1,256]{2,1,0:T(1,128)S(1)} all-to-all(f32[16,1,256]{2,1,0:T(1,128)S(1)} %reshape.1732), channel_id=1, replica_groups=mesh['cuts'=32,'tr'=16] {'tr'}, dimensions={0} | all-to-all | bytes 32768 | tf_op jit(solution)/shard_map/all_to_all | solution.py:42
  143.5 15.0 %all_to_all.56 = f32[16,1,256]{2,1,0:T(1,128)S(1)} all-to-all(f32[16,1,256]{2,1,0:T(1,128)S(1)} %reshape.1734), channel_id=1, replica_groups=mesh['cuts'=32,'tr'=16] {'tr'}, dimensions={0} | all-to-all | bytes 32768 | tf_op jit(solution)/shard_map/all_to_all | solution.py:54
  167.8 4.6 %collective-permute-start.3 = (bf16[512,512]{1,0:T(8,128)(2,1)S(1)}, bf16[512,512]{1,0:T(8,128)(2,1)}, u32[]{:S(2)}, u32[]{:S(2)}) collective-permute-start(bf16[512,512]{1,0:T(8,128)(2,1)S(1)} %fusion.109), channel_id=1, source_target_pairs={{0,480},{16,496},{32,0},{48,16},{64,32},{80,48},{96,64},{112,80},{... | collective-permute-start | bytes 1572872 | tf_op jit(solution)/shard_map/ppermute | solution.py:31
  175.1 4.0 collective-permute-done.3
  179.1 3.8 fusion.118
  189.3 16.2 %all_to_all.57 = bf16[16,32,128]{2,1,0:T(8,128)(2,1)S(1)} all-to-all(bf16[16,32,128]{2,1,0:T(8,128)(2,1)S(1)} %constant_dynamic-update-slice_fusion.16), channel_id=1, replica_groups=mesh['cuts'=32,'tr'=16] {'tr'}, dimensions={0} | all-to-all | bytes 262144 | tf_op jit(solution)/shard_map/all_to_all | solution.py:164
  213.9 4.2 collective-permute-done.5
  218.5 9.9 %while.41 = (s32[]{:T(128)}, f32[4,256,4]{1,0,2:T(4,128)S(1)}, s32[2,2,1024]{2,1,0:T(2,128)S(1)}, s32[4]{0:T(128)S(1)}, f32[2,2,1024]{2,1,0:T(2,128)S(1)}, /*ind...) while((s32[]{:T(128)}, f32[4,256,4]{1,0,2:T(4,128)S(1)}, ...), condition=%wide.region_8.9_spmd, body=%wide.region_5.8_spmd.sunk | while | flops 35309604 | bytes 668095 | solution.py:213
  228.6 18.5 %all_to_all.58 = f32[16,1,256]{2,1,0:T(1,128)S(1)} all-to-all(f32[16,1,256]{2,1,0:T(1,128)S(1)} %reshape.1736), channel_id=1, replica_groups=mesh['cuts'=32,'tr'=16] {'tr'}, dimensions={0} | all-to-all | bytes 32768 | tf_op jit(solution)/shard_map/all_to_all | solution.py:42
  248.0 15.0 %all_to_all.59 = f32[16,1,256]{2,1,0:T(1,128)S(1)} all-to-all(f32[16,1,256]{2,1,0:T(1,128)S(1)} %reshape.1738), channel_id=1, replica_groups=mesh['cuts'=32,'tr'=16] {'tr'}, dimensions={0} | all-to-all | bytes 32768 | tf_op jit(solution)/shard_map/all_to_all | solution.py:54
  266.4 4.8 %collective-permute-start.6 = (bf16[512,512]{1,0:T(8,128)(2,1)S(1)}, bf16[512,512]{1,0:T(8,128)(2,1)}, u32[]{:S(2)}, u32[]{:S(2)}) collective-permute-start(bf16[512,512]{1,0:T(8,128)(2,1)S(1)} %fusion.110), channel_id=1, source_target_pairs={{0,64},{16,80},{32,96},{48,112},{64,128},{80,144},{96,160},{112,17... | collective-permute-start | bytes 1572872 | tf_op jit(solution)/shard_map/ppermute | solution.py:31
  279.9 6.4 %collective-permute-done.7 = bf16[512,512]{1,0:T(8,128)(2,1)} collective-permute-done((bf16[512,512]{1,0:T(8,128)(2,1)S(1)}, bf16[512,512]{1,0:T(8,128)(2,1)}, u32[]{:S(2)}, u32[]{:S(2)}) %collective-permute-start.7) | collective-permute-done | bytes 524320 | tf_op jit(solution)/shard_map/ppermute | solution.py:31
  286.4 3.8 fusion.119
  296.0 15.7 %all_to_all.60 = bf16[16,32,128]{2,1,0:T(8,128)(2,1)S(1)} all-to-all(bf16[16,32,128]{2,1,0:T(8,128)(2,1)S(1)} %constant_dynamic-update-slice_fusion.32), channel_id=1, replica_groups=mesh['cuts'=32,'tr'=16] {'tr'}, dimensions={0} | all-to-all | bytes 262144 | tf_op jit(solution)/shard_map/all_to_all | solution.py:164
  320.3 4.0 collective-permute-done.9
  324.7 9.9 %while.42 = (s32[]{:T(128)}, f32[4,256,4]{1,0,2:T(4,128)S(1)}, s32[2,2,1024]{2,1,0:T(2,128)S(1)}, s32[4]{0:T(128)S(1)}, f32[2,2,1024]{2,1,0:T(2,128)S(1)}, /*ind...) while((s32[]{:T(128)}, f32[4,256,4]{1,0,2:T(4,128)S(1)}, ...), condition=%wide.region_13.14_spmd, body=%wide.region_10.13_spmd.sunk | while | flops 35309604 | bytes 668095 | solution.py:213
  334.8 18.7 %all_to_all.61 = f32[16,1,256]{2,1,0:T(1,128)S(1)} all-to-all(f32[16,1,256]{2,1,0:T(1,128)S(1)} %reshape.1740), channel_id=1, replica_groups=mesh['cuts'=32,'tr'=16] {'tr'}, dimensions={0} | all-to-all | bytes 32768 | tf_op jit(solution)/shard_map/all_to_all | solution.py:42
  354.3 15.0 %all_to_all.62 = f32[16,1,256]{2,1,0:T(1,128)S(1)} all-to-all(f32[16,1,256]{2,1,0:T(1,128)S(1)} %reshape.1742), channel_id=1, replica_groups=mesh['cuts'=32,'tr'=16] {'tr'}, dimensions={0} | all-to-all | bytes 32768 | tf_op jit(solution)/shard_map/all_to_all | solution.py:54
  372.7 6.0 %collective-permute-start.10 = (bf16[512,512]{1,0:T(8,128)(2,1)S(1)}, bf16[512,512]{1,0:T(8,128)(2,1)S(1)}, u32[]{:S(2)}, u32[]{:S(2)}) collective-permute-start(bf16[512,512]{1,0:T(8,128)(2,1)S(1)} %fusion.112), channel_id=1, source_target_pairs={{0,96},{16,112},{32,128},{48,144},{64,160},{80,176},{96,192},{112,... | collective-permute-start | bytes 1572872 | tf_op jit(solution)/shard_map/ppermute | solution.py:31
  385.4 8.2 %collective-permute-done.11 = bf16[512,512]{1,0:T(8,128)(2,1)} collective-permute-done((bf16[512,512]{1,0:T(8,128)(2,1)S(1)}, bf16[512,512]{1,0:T(8,128)(2,1)}, u32[]{:S(2)}, u32[]{:S(2)}) %collective-permute-start.11) | collective-permute-done | bytes 524320 | tf_op jit(solution)/shard_map/ppermute | solution.py:31
  401.0 15.7 %all_to_all.63 = bf16[16,32,128]{2,1,0:T(8,128)(2,1)S(1)} all-to-all(bf16[16,32,128]{2,1,0:T(8,128)(2,1)S(1)} %constant_dynamic-update-slice_fusion.48), channel_id=1, replica_groups=mesh['cuts'=32,'tr'=16] {'tr'}, dimensions={0} | all-to-all | bytes 262144 | tf_op jit(solution)/shard_map/all_to_all | solution.py:164
  424.4 4.2 collective-permute-done.13
  429.0 9.5 %while.43 = (s32[]{:T(128)}, f32[4,256,4]{1,0,2:T(4,128)S(1)}, s32[2,2,1024]{2,1,0:T(2,128)S(1)}, s32[4]{0:T(128)S(1)}, f32[2,2,1024]{2,1,0:T(2,128)S(1)}, /*ind...) while((s32[]{:T(128)}, f32[4,256,4]{1,0,2:T(4,128)S(1)}, ...), condition=%wide.region_18.19_spmd, body=%wide.region_15.18_spmd.sunk | while | flops 35309604 | bytes 668095 | solution.py:213
  438.7 18.7 %all_to_all.64 = f32[16,1,256]{2,1,0:T(1,128)S(1)} all-to-all(f32[16,1,256]{2,1,0:T(1,128)S(1)} %reshape.1744), channel_id=1, replica_groups=mesh['cuts'=32,'tr'=16] {'tr'}, dimensions={0} | all-to-all | bytes 32768 | tf_op jit(solution)/shard_map/all_to_all | solution.py:42
  (800 shorter events, 139.8 us)
Async XLA Ops:
  8.5 17.8 %copy-start.5 = (s32[2,1,2,1024]{3,2,1,0:T(2,128)S(1)}, s32[2,1,2,1024]{3,2,1,0:T(2,128)}, u32[]{:S(2)}) copy-start(s32[2,1,2,1024]{3,2,1,0:T(2,128)} %param.13) | copy-start | bytes 49156
  8.5 17.8 %copy-start.6 = (f32[2,1,2,1024]{3,2,1,0:T(2,128)S(1)}, f32[2,1,2,1024]{3,2,1,0:T(2,128)}, u32[]{:S(2)}) copy-start(f32[2,1,2,1024]{3,2,1,0:T(2,128)} %param.14) | copy-start | bytes 49156
  8.6 17.9 %copy-start.10 = (f32[2,1,1024]{2,1,0:T(1,128)S(1)}, f32[2,1,1024]{2,1,0:T(1,128)}, u32[]{:S(2)}) copy-start(f32[2,1,1024]{2,1,0:T(1,128)} %param.15) | copy-start | bytes 24580
  26.4 10.2 %copy-start.23 = (f32[1,1,512]{2,1,0:T(1,128)}, f32[1,1,512]{2,1,0:T(1,128)S(1)}, u32[]{:S(2)}) copy-start(f32[1,1,512]{2,1,0:T(1,128)S(1)} %get-tuple-element.479) | copy-start | bytes 6148
  26.4 11.4 %copy-start.15 = (f32[1,1,512]{2,1,0:T(1,128)}, f32[1,1,512]{2,1,0:T(1,128)S(1)}, u32[]{:S(2)}) copy-start(f32[1,1,512]{2,1,0:T(1,128)S(1)} %get-tuple-element.481) | copy-start | bytes 6148
  26.5 12.6 %copy-start.19 = (f32[1,1,512]{2,1,0:T(1,128)}, f32[1,1,512]{2,1,0:T(1,128)S(1)}, u32[]{:S(2)}) copy-start(f32[1,1,512]{2,1,0:T(1,128)S(1)} %get-tuple-element.478) | copy-start | bytes 6148
  26.5 14.6 %copy-start.12 = (f32[1,1,512]{2,1,0:T(1,128)}, f32[1,1,512]{2,1,0:T(1,128)S(1)}, u32[]{:S(2)}) copy-start(f32[1,1,512]{2,1,0:T(1,128)S(1)} %get-tuple-element.480) | copy-start | bytes 6148
  27.9 15.1 %copy-start.2 = (bf16[512,128]{1,0:T(8,128)(2,1)}, bf16[512,128]{1,0:T(8,128)(2,1)S(1)}, u32[]{:S(2)}) copy-start(bf16[512,128]{1,0:T(8,128)(2,1)S(1)} %get-tuple-element.491) | copy-start | bytes 393220
  59.3 34.0 %all-to-all-start = ((bf16[16,32,128]{2,1,0:T(8,128)(2,1)}), bf16[16,32,128]{2,1,0:T(8,128)(2,1)S(1)}, u32[]{:S(2)}, u32[]{:S(2)}) async-start(bf16[16,32,128]{2,1,0:T(8,128)(2,1)} %constant_dynamic-update-slice_fusion), calls=%async_computation | async-start | bytes 262144 | tf_op jit(solution)/shard_map/all_to_all | solution.py:164
  93.2 13.9 %copy-start.7 = (f32[2,1,2,1024]{3,2,1,0:T(2,128)S(1)}, f32[2,1,2,1024]{3,2,1,0:T(2,128)}, u32[]{:S(2)}) copy-start(f32[2,1,2,1024]{3,2,1,0:T(2,128)} %param.14) | copy-start | bytes 49156
  97.3 5.2 %collective-permute-start = (bf16[1,2,512]{2,1,0:T(2,128)(2,1)S(1)}, bf16[1,2,512]{2,1,0:T(2,128)(2,1)S(1)}, u32[]{:S(2)}, u32[]{:S(2)}) collective-permute-start(bf16[1,2,512]{2,1,0:T(2,128)(2,1)S(1)} %get-tuple-element.402), channel_id=1, source_target_pairs={{0,1},{1,2},{2,3},{3,4},{4,5},{5,6},{6,7},{7,8},{8,9},{9,10},{10,1... | collective-permute-start | bytes 6152 | tf_op jit(solution)/shard_map/ppermute | solution.py:19
  101.2 5.5 %collective-permute-start.1 = (bf16[1,2,512]{2,1,0:T(2,128)(2,1)S(1)}, bf16[1,2,512]{2,1,0:T(2,128)(2,1)S(1)}, u32[]{:S(2)}, u32[]{:S(2)}) collective-permute-start(bf16[1,2,512]{2,1,0:T(2,128)(2,1)S(1)} %get-tuple-element.403), channel_id=1, source_target_pairs={{1,0},{2,1},{3,2},{4,3},{5,4},{6,5},{7,6},{8,7},{9,8},{10,9},{11,1... | collective-permute-start | bytes 6152 | tf_op jit(solution)/shard_map/ppermute | solution.py:21
  107.1 35.6 %copy-start.11 = (f32[2,1,2,64]{3,2,1,0:T(2,128)S(1)}, f32[2,1,2,64]{3,2,1,0:T(2,128)}, u32[]{:S(2)}) copy-start(f32[2,1,2,64]{3,2,1,0:T(2,128)} %param.16) | copy-start | bytes 3076
  107.2 52.3 %copy-start.24 = (f32[1,1,512]{2,1,0:T(1,128)S(1)}, f32[1,1,512]{2,1,0:T(1,128)}, u32[]{:S(2)}) copy-start(f32[1,1,512]{2,1,0:T(1,128)} %copy-done.23) | copy-start | bytes 6148
  161.8 13.3 %collective-permute-start.2 = (bf16[512,512]{1,0:T(8,128)(2,1)S(1)}, bf16[512,512]{1,0:T(8,128)(2,1)}, u32[]{:S(2)}, u32[]{:S(2)}) collective-permute-start(bf16[512,512]{1,0:T(8,128)(2,1)S(1)} %fusion.108), channel_id=1, source_target_pairs={{0,32},{16,48},{32,64},{48,80},{64,96},{80,112},{96,128},{112,144}... | collective-permute-start | bytes 1572872 | tf_op jit(solution)/shard_map/ppermute | solution.py:31
  166.6 12.5 %copy-start.3 = (bf16[512,128]{1,0:T(8,128)(2,1)S(1)}, bf16[512,128]{1,0:T(8,128)(2,1)}, u32[]{:S(2)}) copy-start(bf16[512,128]{1,0:T(8,128)(2,1)} %copy-done.2) | copy-start | bytes 393220
  167.8 15.2 %copy-start.1 = (f32[1024,64]{0,1:T(8,128)S(1)}, f32[1024,64]{0,1:T(8,128)}, u32[]{:S(2)}) copy-start(f32[1024,64]{0,1:T(8,128)} %copy-done) | copy-start | bytes 786436
  167.8 11.3 %collective-permute-start.3 = (bf16[512,512]{1,0:T(8,128)(2,1)S(1)}, bf16[512,512]{1,0:T(8,128)(2,1)}, u32[]{:S(2)}, u32[]{:S(2)}) collective-permute-start(bf16[512,512]{1,0:T(8,128)(2,1)S(1)} %fusion.109), channel_id=1, source_target_pairs={{0,480},{16,496},{32,0},{48,16},{64,32},{80,48},{96,64},{112,80},{... | collective-permute-start | bytes 1572872 | tf_op jit(solution)/shard_map/ppermute | solution.py:31
  209.5 4.3 collective-permute-start.4
  212.5 5.5 %collective-permute-start.5 = (bf16[1,2,512]{2,1,0:T(2,128)(2,1)S(1)}, bf16[1,2,512]{2,1,0:T(2,128)(2,1)S(1)}, u32[]{:S(2)}, u32[]{:S(2)}) collective-permute-start(bf16[1,2,512]{2,1,0:T(2,128)(2,1)S(1)} %get-tuple-element.401), channel_id=1, source_target_pairs={{1,0},{2,1},{3,2},{4,3},{5,4},{6,5},{7,6},{8,7},{9,8},{10,9},{11,1... | collective-permute-start | bytes 6152 | tf_op jit(solution)/shard_map/ppermute | solution.py:21
  218.4 29.4 %copy-start.9 = (f32[2,1,2,64]{3,2,1,0:T(2,128)S(1)}, f32[2,1,2,64]{3,2,1,0:T(2,128)}, u32[]{:S(2)}) copy-start(f32[2,1,2,64]{3,2,1,0:T(2,128)} %copy-done.8) | copy-start | bytes 3076
  218.4 45.5 %copy-start.25 = (f32[1,1,512]{2,1,0:T(1,128)S(1)}, f32[1,1,512]{2,1,0:T(1,128)}, u32[]{:S(2)}) copy-start(f32[1,1,512]{2,1,0:T(1,128)} %copy-done.23) | copy-start | bytes 6148
  266.4 13.6 %collective-permute-start.6 = (bf16[512,512]{1,0:T(8,128)(2,1)S(1)}, bf16[512,512]{1,0:T(8,128)(2,1)}, u32[]{:S(2)}, u32[]{:S(2)}) collective-permute-start(bf16[512,512]{1,0:T(8,128)(2,1)S(1)} %fusion.110), channel_id=1, source_target_pairs={{0,64},{16,80},{32,96},{48,112},{64,128},{80,144},{96,160},{112,17... | collective-permute-start | bytes 1572872 | tf_op jit(solution)/shard_map/ppermute | solution.py:31
  273.7 12.7 %collective-permute-start.7 = (bf16[512,512]{1,0:T(8,128)(2,1)S(1)}, bf16[512,512]{1,0:T(8,128)(2,1)}, u32[]{:S(2)}, u32[]{:S(2)}) collective-permute-start(bf16[512,512]{1,0:T(8,128)(2,1)S(1)} %fusion.111), channel_id=1, source_target_pairs={{0,448},{16,464},{32,480},{48,496},{64,0},{80,16},{96,32},{112,48}... | collective-permute-start | bytes 1572872 | tf_op jit(solution)/shard_map/ppermute | solution.py:31
  315.8 4.5 collective-permute-start.8
  318.8 5.5 %collective-permute-start.9 = (bf16[1,2,512]{2,1,0:T(2,128)(2,1)S(1)}, bf16[1,2,512]{2,1,0:T(2,128)(2,1)S(1)}, u32[]{:S(2)}, u32[]{:S(2)}) collective-permute-start(bf16[1,2,512]{2,1,0:T(2,128)(2,1)S(1)} %get-tuple-element.399), channel_id=1, source_target_pairs={{1,0},{2,1},{3,2},{4,3},{5,4},{6,5},{7,6},{8,7},{9,8},{10,9},{11,1... | collective-permute-start | bytes 6152 | tf_op jit(solution)/shard_map/ppermute | solution.py:21
  324.7 45.6 %copy-start.26 = (f32[1,1,512]{2,1,0:T(1,128)S(1)}, f32[1,1,512]{2,1,0:T(1,128)}, u32[]{:S(2)}) copy-start(f32[1,1,512]{2,1,0:T(1,128)} %copy-done.23) | copy-start | bytes 6148
  372.7 12.7 %collective-permute-start.10 = (bf16[512,512]{1,0:T(8,128)(2,1)S(1)}, bf16[512,512]{1,0:T(8,128)(2,1)S(1)}, u32[]{:S(2)}, u32[]{:S(2)}) collective-permute-start(bf16[512,512]{1,0:T(8,128)(2,1)S(1)} %fusion.112), channel_id=1, source_target_pairs={{0,96},{16,112},{32,128},{48,144},{64,160},{80,176},{96,192},{112,... | collective-permute-start | bytes 1572872 | tf_op jit(solution)/shard_map/ppermute | solution.py:31
  381.2 12.4 %collective-permute-start.11 = (bf16[512,512]{1,0:T(8,128)(2,1)S(1)}, bf16[512,512]{1,0:T(8,128)(2,1)}, u32[]{:S(2)}, u32[]{:S(2)}) collective-permute-start(bf16[512,512]{1,0:T(8,128)(2,1)S(1)} %fusion.113), channel_id=1, source_target_pairs={{0,416},{16,432},{32,448},{48,464},{64,480},{80,496},{96,0},{112,1... | collective-permute-start | bytes 1572872 | tf_op jit(solution)/shard_map/ppermute | solution.py:31
  399.0 17.7 %copy-start.4 = (bf16[512,2048]{1,0:T(8,128)(2,1)S(1)}, bf16[512,2048]{1,0:T(8,128)(2,1)}, u32[]{:S(2)}) copy-start(bf16[512,2048]{1,0:T(8,128)(2,1)} %get-tuple-element.420) | copy-start | bytes 6291460
  420.1 4.3 collective-permute-start.12
  423.1 5.5 %collective-permute-start.13 = (bf16[1,2,512]{2,1,0:T(2,128)(2,1)S(1)}, bf16[1,2,512]{2,1,0:T(2,128)(2,1)S(1)}, u32[]{:S(2)}, u32[]{:S(2)}) collective-permute-start(bf16[1,2,512]{2,1,0:T(2,128)(2,1)S(1)} %get-tuple-element.397), channel_id=1, source_target_pairs={{1,0},{2,1},{3,2},{4,3},{5,4},{6,5},{7,6},{8,7},{9,8},{10,9},{11,1... | collective-permute-start | bytes 6152 | tf_op jit(solution)/shard_map/ppermute | solution.py:21
  (10 other events, 25.4 us)
